TPU v7x, 32 devices: a whole 2x2x4 slice. The times are simulated.
32 devices in a mesh: section: 4 (over y, x), cp: 4 (over z), tp: 2 (over core).
Axes of the slice: x: 2, y: 2, z: 4, core: 2. Of those that a mesh axis runs over, the one named last changes fastest.
Arguments:
- acts: bfloat16 [4, 512, 8192], P('section', 'cp', 'tp'), may hold values from -16 to 16
- keys: bfloat16 [4, 512, 1024], P('section', 'cp', 'tp'), may hold values from -4 to 4
- values: bfloat16 [4, 512, 1024], P('section', 'cp', 'tp'), may hold values from -6 to 6
- grads: bfloat16 [4, 512, 8192], P('section', 'cp', 'tp'), may hold values from -6 to 6
- docs: int32 [4, 512], P('section'), may hold values from 0 to 7, never falling along the last dimension, each value on 1 to 256 neighbouring positions
- order: int32 [4, 512], P('section'), may hold values from 0 to 511, each once within a row
Outputs:
- outputs: bfloat16 [4, 512, 8192], P('section', 'cp', 'tp')
- grad_query: bfloat16 [4, 512, 8192], P('section', 'cp', 'tp')
- grad_keys: bfloat16 [4, 512, 1024], P('section', 'cp', 'tp')
- grad_values: bfloat16 [4, 512, 1024], P('section', 'cp', 'tp')
Inputs may be any that keep to these rules, and one draw needn't show every extreme that they name: `docs`: along positions of one section the document numbers never fall; each document holds 1 to 256 tokens. `order`: each section's row holds every position once.
All inputs are finite; a program needn't handle non-finite values.
Results may differ from a plain program's by a relative error of at most 0.0061.
Values may be sent and summed in bfloat16 or wider, within the bound.
A program may use at most 64 MiB of HBM per device.

v0:
```python
import jax
import jax.numpy as jnp
from jax import lax
from jax.sharding import PartitionSpec as P

HEAD = 128


def passed_along(block, axis, distance):
    devices = range(lax.axis_size(axis))
    route = [((i - distance) % len(devices), i) for i in devices]
    return lax.ppermute(block, axis, route)


def split_heads(block, kv_count):
    tokens = block.shape[0]
    group = block.shape[1] // (kv_count * HEAD)
    return (
        block.reshape(tokens, kv_count, group, HEAD)
        .transpose(1, 2, 0, 3)
        .reshape(kv_count, group * tokens, HEAD)
    )


def join_heads(rows, tokens):
    kv_count = rows.shape[0]
    group = rows.shape[1] // tokens
    return (
        rows.reshape(kv_count, group, tokens, HEAD)
        .transpose(2, 0, 1, 3)
        .reshape(tokens, kv_count * group * HEAD)
    )


def forward_part(flat_q, key, value, allowed):
    scale = HEAD ** (-0.5)
    rows_q = allowed.shape[0]
    scores = (
        lax.dot_general(flat_q, key, (((1,), (1,)), ((), ())), preferred_element_type=jnp.float32)
        * scale
    )
    scores = scores.reshape(-1, rows_q, key.shape[0])
    scores = jnp.where(allowed[None], scores, -jnp.inf)
    peak = jnp.max(scores, axis=2, keepdims=True)
    expd = jnp.exp(scores - peak)
    probs = (expd / jnp.sum(expd, axis=2, keepdims=True)).astype(jnp.bfloat16)
    probs = probs.reshape(flat_q.shape[0], key.shape[0])
    attended = jnp.dot(probs, value, preferred_element_type=jnp.float32)
    return (probs, attended)


def backward_part(probs, attended, flat_g, key, value):
    scale = HEAD ** (-0.5)
    delta = jnp.sum(flat_g.astype(jnp.float32) * attended, axis=1, keepdims=True)
    dprob = lax.dot_general(
        flat_g, value, (((1,), (1,)), ((), ())), preferred_element_type=jnp.float32
    )
    dscore = (probs.astype(jnp.float32) * (dprob - delta)).astype(jnp.bfloat16)
    dquery = jnp.dot(dscore, key, preferred_element_type=jnp.float32) * scale
    return (dscore, dquery)


def key_terms(probs, dscore, flat_q, flat_g):
    scale = HEAD ** (-0.5)
    dkey = (
        lax.dot_general(
            dscore, flat_q, (((0,), (0,)), ((), ())), preferred_element_type=jnp.float32
        )
        * scale
    )
    dvalue = lax.dot_general(
        probs, flat_g, (((0,), (0,)), ((), ())), preferred_element_type=jnp.float32
    )
    return (dkey, dvalue)


def stack_terms(dkeys, dvalues):
    count = dkeys.shape[1]
    return jnp.concatenate(
        [
            dkeys.transpose(1, 0, 2).reshape(count, -1),
            dvalues.transpose(1, 0, 2).reshape(count, -1),
        ],
        axis=1,
    )


def on_device(acts, keys, values, grads, docs, order):
    tok = acts.shape[1]
    kv_count = keys.shape[2] // HEAD
    width = kv_count * HEAD
    query = passed_along(acts, "section", 1)[0]
    cotan = passed_along(grads, "section", -1)[0]
    key_all, value_all = (
        lax.all_gather(keys[0], "cp", axis=0, tiled=True),
        lax.all_gather(values[0], "cp", axis=0, tiled=True),
    )
    positions = order[0]
    doc_all = jnp.take(docs[0], positions)
    first = lax.axis_index("cp") * tok
    my_pos = lax.dynamic_slice_in_dim(positions, first, tok)
    my_doc = lax.dynamic_slice_in_dim(doc_all, first, tok)
    allowed = (my_doc[:, None] == doc_all[None, :]) & (positions[None, :] <= my_pos[:, None])
    q_rows = split_heads(query, kv_count)
    k_heads = key_all.reshape(-1, kv_count, HEAD).transpose(1, 0, 2)
    v_heads = value_all.reshape(-1, kv_count, HEAD).transpose(1, 0, 2)
    probs, attended = lax.map(
        lambda parts: forward_part(parts[0], parts[1], parts[2], allowed),
        (q_rows, k_heads, v_heads),
    )
    outputs = (query.astype(jnp.float32) + join_heads(attended, tok)).astype(jnp.bfloat16)
    g_rows = split_heads(cotan, kv_count)
    dscores, dqueries = lax.map(
        lambda parts: backward_part(parts[0], parts[1], parts[2], parts[3], parts[4]),
        (probs, attended, g_rows, k_heads, v_heads),
    )
    grad_query = (cotan.astype(jnp.float32) + join_heads(dqueries, tok)).astype(jnp.bfloat16)
    dkeys, dvalues = jax.vmap(key_terms)(probs, dscores, q_rows, g_rows)
    summed = lax.psum_scatter(stack_terms(dkeys, dvalues), "cp", scatter_dimension=0, tiled=True)
    grad_keys = summed[:, :width].astype(jnp.bfloat16)
    grad_values = summed[:, width:].astype(jnp.bfloat16)
    return (outputs[None], grad_query[None], grad_keys[None], grad_values[None])


def solution(mesh):
    placed = (
        P("section", "cp", "tp"),
        P("section", "cp", "tp"),
        P("section", "cp", "tp"),
        P("section", "cp", "tp"),
        P("section", None),
        P("section", None),
    )
    return jax.shard_map(
        on_device,
        mesh=mesh,
        in_specs=placed,
        out_specs=(
            P("section", "cp", "tp"),
            P("section", "cp", "tp"),
            P("section", "cp", "tp"),
            P("section", "cp", "tp"),
        ),
        check_vma=False,
    )
```

profile of v0, /device:TPU:0, one launch (start us, length us, event | category | flops | bytes accessed | tf_op | source)
XLA Modules:
  0.0 176.0 jit_solution(15219660777080566842)
XLA Ops:
  7.2 3.0 %collective-permute-start = (bf16[1,128,4096]{2,1,0:T(8,128)(2,1)}, bf16[1,128,4096]{2,1,0:T(8,128)(2,1)S(1)}, u32[]{:S(2)}, u32[]{:S(2)}) collective-permute-start(bf16[1,128,4096]{2,1,0:T(8,128)(2,1)} %param.10), channel_id=1, source_target_pairs={{24,0},{0,8},{8,16},{16,24},{25,1},{1,9},{9,17},{17,25},{26,2},{2,... | collective-permute-start | bytes 3145736 | tf_op jit(solution)/shard_map/ppermute | solution.py:12
  12.3 15.2 %all-gather = bf16[1,512,512]{1,2,0:T(8,128)(2,1)S(1)} all-gather(bf16[1,128,512]{1,2,0:T(8,128)(2,1)S(1)} %copy.22), channel_id=2, replica_groups=mesh['section'=4,'cp'=4,'tp'=2] {'cp'}, dimensions={1}, use_global_device_ids=true | all-gather | bytes 655360 | tf_op jit(solution)/shard_map/all_gather | solution.py:95
  29.5 14.3 %all-gather.1 = bf16[1,512,512]{1,2,0:T(8,128)(2,1)S(1)} all-gather(bf16[1,128,512]{1,2,0:T(8,128)(2,1)S(1)} %copy.23), channel_id=3, replica_groups=mesh['section'=4,'cp'=4,'tp'=2] {'cp'}, dimensions={1}, use_global_device_ids=true | all-gather | bytes 655360 | tf_op jit(solution)/shard_map/all_gather | solution.py:96
  44.9 3.5 %gather_fusion = s32[512]{0:T(512)S(1)} fusion(s32[512]{0:T(512)S(1)} %bitcast.141, s32[1024]{0:T(1024)S(1)} %pad_clamp_fusion), kind=kCustom, calls=%fused_computation | custom fusion | bytes 6144 | tf_op jit(solution)/shard_map/jit(_take)/gather | solution.py:99
  51.2 1.5 broadcast.70.clone
  52.7 23.3 %while.26 = (s32[]{:T(128)}, bf16[4,1024,512]{1,2,0:T(8,128)(2,1)}, f32[4,1024,128]{2,1,0:T(8,128)}, bf16[4,1024,128]{1,2,0:T(8,128)(2,1)S(1)}, bf16[4,512,128]{...) while((s32[]{:T(128)}, bf16[4,1024,512]{1,2,0:T(8,128)(2,1)}, ...), condition=%wide.region_3.4_spmd.clone, body=%wide.region_0.3_spmd.clone.sunk | while | flops 274397184 | bytes 11701869 | solution.py:107
  53.2 1.5 fusion.43
  55.0 2.3 %fusion.45 = f32[4,1024,128]{2,1,0:T(8,128)} fusion(f32[4,1024,128]{2,1,0:T(8,128)} %get-tuple-element.324, s32[]{:T(128)} %get-tuple-element.322, bf16[4,512,128]{2,1,0:T(8,128)(2,1)} %get-tuple-element.338, f32[1024,512]{0,1:T(8,128)S(1)} %get-tuple-element.309, f32[1024]{0:T(1024)S(1)} %fusion.44, f32[1024]{0:T(1024)S(1)} %get-tuple-element.310), kind=kOutput, calls=%fused_computation.24.clone.1 | convolution fusion | flops 135790592 | bytes 2761728 | tf_op jit(solution)/shard_map/while/body/eval_jaxpr/dot_general | solution.py:48
  60.8 2.3 %fusion.45 = f32[4,1024,128]{2,1,0:T(8,128)} fusion(f32[4,1024,128]{2,1,0:T(8,128)} %get-tuple-element.324, s32[]{:T(128)} %get-tuple-element.322, bf16[4,512,128]{2,1,0:T(8,128)(2,1)} %get-tuple-element.338, f32[1024,512]{0,1:T(8,128)S(1)} %get-tuple-element.309, f32[1024]{0:T(1024)S(1)} %fusion.44, f32[1024]{0:T(1024)S(1)} %get-tuple-element.310), kind=kOutput, calls=%fused_computation.24.clone.1 | convolution fusion | flops 135790592 | bytes 2761728 | tf_op jit(solution)/shard_map/while/body/eval_jaxpr/dot_general | solution.py:48
  64.8 1.5 fusion.43
  66.6 2.2 %fusion.45 = f32[4,1024,128]{2,1,0:T(8,128)} fusion(f32[4,1024,128]{2,1,0:T(8,128)} %get-tuple-element.324, s32[]{:T(128)} %get-tuple-element.322, bf16[4,512,128]{2,1,0:T(8,128)(2,1)} %get-tuple-element.338, f32[1024,512]{0,1:T(8,128)S(1)} %get-tuple-element.309, f32[1024]{0:T(1024)S(1)} %fusion.44, f32[1024]{0:T(1024)S(1)} %get-tuple-element.310), kind=kOutput, calls=%fused_computation.24.clone.1 | convolution fusion | flops 135790592 | bytes 2761728 | tf_op jit(solution)/shard_map/while/body/eval_jaxpr/dot_general | solution.py:48
  70.6 1.5 fusion.43
  72.4 2.2 %fusion.45 = f32[4,1024,128]{2,1,0:T(8,128)} fusion(f32[4,1024,128]{2,1,0:T(8,128)} %get-tuple-element.324, s32[]{:T(128)} %get-tuple-element.322, bf16[4,512,128]{2,1,0:T(8,128)(2,1)} %get-tuple-element.338, f32[1024,512]{0,1:T(8,128)S(1)} %get-tuple-element.309, f32[1024]{0:T(1024)S(1)} %fusion.44, f32[1024]{0:T(1024)S(1)} %get-tuple-element.310), kind=kOutput, calls=%fused_computation.24.clone.1 | convolution fusion | flops 135790592 | bytes 2761728 | tf_op jit(solution)/shard_map/while/body/eval_jaxpr/dot_general | solution.py:48
  80.2 4.8 %fusion.24 = f32[4,512,128]{1,2,0:T(8,128)} fusion(bf16[4,1024,512]{1,2,0:T(8,128)(2,1)} %get-tuple-element.347, bf16[4,1024,128]{1,2,0:T(8,128)(2,1)S(1)} %reshape.120), kind=kOutput, calls=%fused_computation.51 | convolution fusion | flops 536870912 | bytes 6291456 | tf_op jit(solution)/shard_map/vmap()/dot_general | solution.py:71
  85.0 1.5 broadcast.70
  86.4 31.5 %while.25 = (s32[]{:T(128)}, bf16[4,1024,512]{2,1,0:T(8,128)(2,1)}, f32[4,1024,128]{2,1,0:T(8,128)}, bf16[4,1024,512]{1,2,0:T(8,128)(2,1)}, bf16[4,1024,128]{1,2...) while((s32[]{:T(128)}, bf16[4,1024,512]{2,1,0:T(8,128)(2,1)}, ...), condition=%wide.region_6.7_spmd, body=%wide.region_4.6_spmd.sunk | while | flops 271055872 | bytes 11283049 | solution.py:113
  89.8 2.4 %bitcast_dynamic-update-slice_fusion.4 = (bf16[4,1024,512]{2,1,0:T(8,128)(2,1)}, bf16[1024,512]{1,0:T(8,128)(2,1)S(1)}) fusion(bf16[4,1024,512]{2,1,0:T(8,128)(2,1)} %get-tuple-element.354, s32[]{:T(128)} %get-tuple-element.353, f32[1024]{0:T(1024)S(1)} %fusion.40, bf16[4,512,128]{2,1,0:T(8,128)(2,1)} %get-tuple-element.367, ...), kind=kOutput, calls=%fused_computation.7.clone.1 | convolution fusion | flops 136314880 | bytes 3544576 | tf_op jit(solution)/shard_map/while/body/eval_jaxpr/dot_general | solution.py:55
  92.1 2.2 %fusion.41 = f32[4,1024,128]{2,1,0:T(8,128)} fusion(f32[4,1024,128]{2,1,0:T(8,128)} %get-tuple-element.355, s32[]{:T(128)} %get-tuple-element.353, bf16[1024,512]{1,0:T(8,128)(2,1)S(1)} %get-tuple-element.298, bf16[4,512,128]{2,1,0:T(8,128)(2,1)} %get-tuple-element.369), kind=kOutput, calls=%fused_computation.6.clone.1 | convolution fusion | flops 134348800 | bytes 1704960 | tf_op jit(solution)/shard_map/while/body/eval_jaxpr/dot_general | solution.py:59
  97.6 2.4 %bitcast_dynamic-update-slice_fusion.4 = (bf16[4,1024,512]{2,1,0:T(8,128)(2,1)}, bf16[1024,512]{1,0:T(8,128)(2,1)S(1)}) fusion(bf16[4,1024,512]{2,1,0:T(8,128)(2,1)} %get-tuple-element.354, s32[]{:T(128)} %get-tuple-element.353, f32[1024]{0:T(1024)S(1)} %fusion.40, bf16[4,512,128]{2,1,0:T(8,128)(2,1)} %get-tuple-element.367, ...), kind=kOutput, calls=%fused_computation.7.clone.1 | convolution fusion | flops 136314880 | bytes 3544576 | tf_op jit(solution)/shard_map/while/body/eval_jaxpr/dot_general | solution.py:55
  100.1 2.1 %fusion.41 = f32[4,1024,128]{2,1,0:T(8,128)} fusion(f32[4,1024,128]{2,1,0:T(8,128)} %get-tuple-element.355, s32[]{:T(128)} %get-tuple-element.353, bf16[1024,512]{1,0:T(8,128)(2,1)S(1)} %get-tuple-element.298, bf16[4,512,128]{2,1,0:T(8,128)(2,1)} %get-tuple-element.369), kind=kOutput, calls=%fused_computation.6.clone.1 | convolution fusion | flops 134348800 | bytes 1704960 | tf_op jit(solution)/shard_map/while/body/eval_jaxpr/dot_general | solution.py:59
  105.5 2.4 %bitcast_dynamic-update-slice_fusion.4 = (bf16[4,1024,512]{2,1,0:T(8,128)(2,1)}, bf16[1024,512]{1,0:T(8,128)(2,1)S(1)}) fusion(bf16[4,1024,512]{2,1,0:T(8,128)(2,1)} %get-tuple-element.354, s32[]{:T(128)} %get-tuple-element.353, f32[1024]{0:T(1024)S(1)} %fusion.40, bf16[4,512,128]{2,1,0:T(8,128)(2,1)} %get-tuple-element.367, ...), kind=kOutput, calls=%fused_computation.7.clone.1 | convolution fusion | flops 136314880 | bytes 3544576 | tf_op jit(solution)/shard_map/while/body/eval_jaxpr/dot_general | solution.py:55
  107.9 2.1 %fusion.41 = f32[4,1024,128]{2,1,0:T(8,128)} fusion(f32[4,1024,128]{2,1,0:T(8,128)} %get-tuple-element.355, s32[]{:T(128)} %get-tuple-element.353, bf16[1024,512]{1,0:T(8,128)(2,1)S(1)} %get-tuple-element.298, bf16[4,512,128]{2,1,0:T(8,128)(2,1)} %get-tuple-element.369), kind=kOutput, calls=%fused_computation.6.clone.1 | convolution fusion | flops 134348800 | bytes 1704960 | tf_op jit(solution)/shard_map/while/body/eval_jaxpr/dot_general | solution.py:59
  113.4 2.4 %bitcast_dynamic-update-slice_fusion.4 = (bf16[4,1024,512]{2,1,0:T(8,128)(2,1)}, bf16[1024,512]{1,0:T(8,128)(2,1)S(1)}) fusion(bf16[4,1024,512]{2,1,0:T(8,128)(2,1)} %get-tuple-element.354, s32[]{:T(128)} %get-tuple-element.353, f32[1024]{0:T(1024)S(1)} %fusion.40, bf16[4,512,128]{2,1,0:T(8,128)(2,1)} %get-tuple-element.367, ...), kind=kOutput, calls=%fused_computation.7.clone.1 | convolution fusion | flops 136314880 | bytes 3544576 | tf_op jit(solution)/shard_map/while/body/eval_jaxpr/dot_general | solution.py:55
  115.8 2.1 %fusion.41 = f32[4,1024,128]{2,1,0:T(8,128)} fusion(f32[4,1024,128]{2,1,0:T(8,128)} %get-tuple-element.355, s32[]{:T(128)} %get-tuple-element.353, bf16[1024,512]{1,0:T(8,128)(2,1)S(1)} %get-tuple-element.298, bf16[4,512,128]{2,1,0:T(8,128)(2,1)} %get-tuple-element.369), kind=kOutput, calls=%fused_computation.6.clone.1 | convolution fusion | flops 134348800 | bytes 1704960 | tf_op jit(solution)/shard_map/while/body/eval_jaxpr/dot_general | solution.py:59
  117.9 3.2 %convolution_multiply_fusion.1 = f32[4,512,128]{1,2,0:T(8,128)S(1)} fusion(bf16[4,1024,128]{1,2,0:T(8,128)(2,1)} %copy-done.3, bf16[4,1024,512]{2,1,0:T(8,128)(2,1)} %get-tuple-element.88), kind=kOutput, calls=%fused_computation.40 | convolution fusion | flops 537133056 | bytes 6291456 | tf_op jit(solution)/shard_map/vmap()/dot_general | solution.py:66
  122.7 1.5 pad_maximum_fusion
  124.3 1.6 copy-done.1
  125.9 2.5 %copy.48 = f32[4,8,128,128]{3,1,0,2:T(8,128)} copy(f32[4,8,128,128]{3,2,1,0:T(8,128)S(1)} %bitcast.143) | data formatting | bytes 4194304 | tf_op jit(solution)/shard_map/reshape | solution.py:29
  128.4 1.9 %reshape.122 = f32[1,128,4096]{2,1,0:T(8,128)S(1)} reshape(f32[128,4,8,128]{3,2,1,0:T(8,128)} %bitcast.144) | data formatting | bytes 4194304 | tf_op jit(solution)/shard_map/reshape | solution.py:31
  130.3 4.1 %copy.49 = f32[4,8,128,128]{3,1,0,2:T(8,128)} copy(f32[4,8,128,128]{3,2,1,0:T(8,128)} %bitcast.19) | data formatting | bytes 4194304 | tf_op jit(solution)/shard_map/reshape | solution.py:29
  134.4 2.9 %reshape.119 = f32[1,128,4096]{2,1,0:T(8,128)} reshape(f32[128,4,8,128]{3,2,1,0:T(8,128)} %bitcast.145) | data formatting | bytes 4194304 | tf_op jit(solution)/shard_map/reshape | solution.py:31
  140.7 26.7 %reduce-scatter.2.cloned.1.call-done = f32[128,1024]{1,0:T(8,128)} async-done(((f32[512,1024]{1,0:T(8,128)}), f32[128,1024]{1,0:T(8,128)}) %reduce-scatter.2.cloned.1.call-update) | async-done | bytes 524304 | tf_op jit(solution)/shard_map/reduce_scatter | solution.py:119
  (85 shorter events, 41.9 us)
Async XLA Ops:
  7.2 37.7 %copy-start = (s32[1,512]{1,0:T(1,128)S(1)}, s32[1,512]{1,0:T(1,128)}, u32[]{:S(2)}) copy-start(s32[1,512]{1,0:T(1,128)} %param.14) | copy-start | bytes 6148
  7.2 37.7 %copy-start.9 = (s32[1,512]{1,0:T(1,128)S(1)}, s32[1,512]{1,0:T(1,128)}, u32[]{:S(2)}) copy-start(s32[1,512]{1,0:T(1,128)} %param.15) | copy-start | bytes 6148
  7.2 160.2 %reduce-scatter.2.cloned.1.call-start = ((), (), s32[]{:S(2)}) async-start(), calls=%async_computation.1 | async-start | bytes 2621440 | tf_op jit(solution)/shard_map/reduce_scatter | solution.py:119
  7.2 41.3 %collective-permute-start = (bf16[1,128,4096]{2,1,0:T(8,128)(2,1)}, bf16[1,128,4096]{2,1,0:T(8,128)(2,1)S(1)}, u32[]{:S(2)}, u32[]{:S(2)}) collective-permute-start(bf16[1,128,4096]{2,1,0:T(8,128)(2,1)} %param.10), channel_id=1, source_target_pairs={{24,0},{0,8},{8,16},{16,24},{25,1},{1,9},{9,17},{17,25},{26,2},{2,... | collective-permute-start | bytes 3145736 | tf_op jit(solution)/shard_map/ppermute | solution.py:12
  10.3 65.8 %collective-permute-start.1 = (bf16[1,128,4096]{2,1,0:T(8,128)(2,1)}, bf16[1,128,4096]{2,1,0:T(8,128)(2,1)S(1)}, u32[]{:S(2)}, u32[]{:S(2)}) collective-permute-start(bf16[1,128,4096]{2,1,0:T(8,128)(2,1)} %param.13), channel_id=1, source_target_pairs={{8,0},{16,8},{24,16},{0,24},{9,1},{17,9},{25,17},{1,25},{10,2},{18... | collective-permute-start | bytes 3145736 | tf_op jit(solution)/shard_map/ppermute | solution.py:12
  48.5 1.0 copy-start.4
  76.0 3.7 %copy-start.3 = (bf16[4,1024,128]{1,2,0:T(8,128)(2,1)}, bf16[4,1024,128]{1,2,0:T(8,128)(2,1)S(1)}, u32[]{:S(2)}) copy-start(bf16[4,1024,128]{1,2,0:T(8,128)(2,1)S(1)} %get-tuple-element.374) | copy-start | bytes 3145732
  76.0 1.0 copy-start.6
  121.2 1.2 copy-start.8
  124.3 1.6 copy-start.1
  134.4 2.9 %copy-start.7 = (bf16[1,128,4096]{2,1,0:T(8,128)(2,1)S(1)}, bf16[1,128,4096]{2,1,0:T(8,128)(2,1)}, u32[]{:S(2)}) copy-start(bf16[1,128,4096]{2,1,0:T(8,128)(2,1)} %copy-done.6) | copy-start | bytes 3145732
  137.3 2.0 %copy-start.2 = (f32[1,128,4096]{2,1,0:T(8,128)S(1)}, f32[1,128,4096]{2,1,0:T(8,128)}, u32[]{:S(2)}) copy-start(f32[1,128,4096]{2,1,0:T(8,128)} %reshape.119) | copy-start | bytes 6291460
  137.3 2.2 %copy-start.5 = (bf16[1,128,4096]{2,1,0:T(8,128)(2,1)S(1)}, bf16[1,128,4096]{2,1,0:T(8,128)(2,1)}, u32[]{:S(2)}) copy-start(bf16[1,128,4096]{2,1,0:T(8,128)(2,1)} %copy-done.4) | copy-start | bytes 3145732
Sparse Core Ops, SparseCore 0:
  124.4 42.9 reduce-scatter.1
where the time goes:
time: 177 us; the launch traced here: 176 us
  local copies, waits for them, and re-layouts  42.9 us (24%)
  matrix products  41 us (23%)
  blocking collectives  29.5 us (17%)
  waiting for transfers between devices  26.7 us (15%)
  other arithmetic  17.5 us (10%)
  between operations  14.2 us (8%)
  starting transfers between devices  4.08 us (2%)
    reduce_scatter x1, waiting for transfers between devices, on_device(): lax.psum_scatter(stack_terms(dkeys, dvalues), 'cp', scatter_dimension=0,...  26.7 us
    all_gather x1, blocking collectives, on_device(): lax.all_gather(keys[0], 'cp', axis=0, tiled=True)  15.2 us
    all_gather x1, blocking collectives, on_device(): lax.all_gather(values[0], 'cp', axis=0, tiled=True)  14.3 us
    unnamed x26, local copies, waits for them, and re-layouts  11 us
    dot_general x4, matrix products, backward_part(): lax.dot_general(flat_g, value, (((1,), (1,)), ((), ())), preferred_elemen...  9.64 us
    dot_general x4, matrix products, forward_part(): attended = jnp.dot(probs, value, preferred_element_type=jnp.float32)  9 us
    dot_general x4, matrix products, backward_part(): dquery = jnp.dot(dscore, key, preferred_element_type=jnp.float32) * scale  8.56 us
    dynamic_slice x8, local copies, waits for them, and re-layouts, on_device(): lax.map(lambda parts: backward_part(parts[0], parts[1], parts[2], parts[3...  7.37 us
  transfers between devices with their start and end apart: 3, of which 1 were waited for; matrix products, arithmetic and copies ran while one was open for 27% of the time, Pallas kernels for 0%

commit v1 on v0

--- a/solution.py
+++ b/solution.py
@@ -4,6 +4,23 @@
 from jax.sharding import PartitionSpec as P
 
 HEAD = 128
+
+
+def joined_along(pieces, dim):
+    pieces = jnp.moveaxis(pieces, 0, dim)
+    dims = pieces.shape
+    return pieces.reshape(*dims[:dim], dims[dim] * dims[dim + 1], *dims[dim + 2 :])
+
+
+def ring_gather(shard, axis, dim):
+    count = lax.axis_size(axis)
+    right = [(i, (i + 1) % count) for i in range(count)]
+    pieces = [shard]
+    while len(pieces) < count:
+        pieces.append(lax.ppermute(pieces[-1], axis, right))
+    place = lax.axis_index(axis)
+    pieces = jnp.stack(pieces)[(place - jnp.arange(count)) % count]
+    return joined_along(pieces, dim)
 
 
 def passed_along(block, axis, distance):
@@ -93,7 +110,7 @@
     cotan = passed_along(grads, "section", -1)[0]
     key_all, value_all = (
         lax.all_gather(keys[0], "cp", axis=0, tiled=True),
-        lax.all_gather(values[0], "cp", axis=0, tiled=True),
+        ring_gather(values[0], "cp", 0),
     )
     positions = order[0]
     doc_all = jnp.take(docs[0], positions)

time: 177 us -> 171 us (0.966)
  blocking collectives: 29.5 us -> 15.7 us
  waiting for transfers between devices: 26.7 us -> 30.5 us
  starting transfers between devices: 4.08 us -> 7.75 us
    all_gather x1 -> x0, blocking collectives: 14.3 us -> none  [on_device(): lax.all_gather(values[0], 'cp', axis=0, tiled=True)]
    ppermute x0 -> x3, waiting for transfers between devices: none -> 5.64 us  [ring_gather(): pieces.append(lax.ppermute(pieces[-1], axis, right))]
    ppermute x0 -> x3, starting transfers between devices: none -> 4.79 us  [ring_gather(): pieces.append(lax.ppermute(pieces[-1], axis, right))]
    reduce_scatter x1, waiting for transfers between devices: 26.7 us -> 24.8 us  [on_device(): lax.psum_scatter(stack_terms(dkeys, dvalues), 'cp', scatter_dimension=0,...]
    unnamed x26 -> x27, local copies, waits for them, and re-layouts: 11 us -> 9.84 us
  transfers between devices with their start and end apart: 3 -> 6, of which waited for: 1 -> 2; matrix products, arithmetic and copies ran while one was open for 27% -> 28% of each run, Pallas kernels for 0% -> 0%
where the time goes in v1:
time: 171 us; the launch traced here: 170 us
  local copies, waits for them, and re-layouts  42.2 us (25%)
  matrix products  41 us (24%)
  waiting for transfers between devices  30.5 us (18%)
  other arithmetic  18.2 us (11%)
  blocking collectives  15.7 us (9%)
  between operations  14.3 us (8%)
  starting transfers between devices  7.75 us (5%)
    reduce_scatter x1, waiting for transfers between devices, on_device(): lax.psum_scatter(stack_terms(dkeys, dvalues), 'cp', scatter_dimension=0,...  24.8 us
    all_gather x1, blocking collectives, on_device(): lax.all_gather(keys[0], 'cp', axis=0, tiled=True)  15.7 us
    unnamed x27, local copies, waits for them, and re-layouts  9.84 us
    dot_general x4, matrix products, backward_part(): lax.dot_general(flat_g, value, (((1,), (1,)), ((), ())), preferred_elemen...  9.64 us
    dot_general x4, matrix products, forward_part(): attended = jnp.dot(probs, value, preferred_element_type=jnp.float32)  9 us
    dot_general x4, matrix products, backward_part(): dquery = jnp.dot(dscore, key, preferred_element_type=jnp.float32) * scale  8.54 us
    dynamic_slice x8, local copies, waits for them, and re-layouts, on_device(): lax.map(lambda parts: backward_part(parts[0], parts[1], parts[2], parts[3...  7.37 us
    reshape x2, local copies, waits for them, and re-layouts, join_heads(): rows.reshape(kv_count, group, tokens, HEAD).transpose(2, 0, 1, 3)  6.65 us
  transfers between devices with their start and end apart: 6, of which 2 were waited for; matrix products, arithmetic and copies ran while one was open for 28% of the time, Pallas kernels for 0%

profile of v1, /device:TPU:0, one launch (start us, length us, event | category | flops | bytes accessed | tf_op | source)
XLA Modules:
  0.0 170.0 jit_solution(8339416232269846386)
XLA Ops:
  7.2 3.1 %collective-permute-start.1 = (bf16[128,512]{1,0:T(8,128)(2,1)}, bf16[128,512]{1,0:T(8,128)(2,1)S(1)}, u32[]{:S(2)}, u32[]{:S(2)}) collective-permute-start(bf16[128,512]{1,0:T(8,128)(2,1)} %bitcast.162), channel_id=1, source_target_pairs={{0,2},{2,4},{4,6},{6,0},{1,3},{3,5},{5,7},{7,1},{8,10},{10,12},{12... | collective-permute-start | bytes 393224 | tf_op jit(solution)/shard_map/ppermute | solution.py:20
  10.4 1.5 collective-permute-start
  15.0 3.5 %gather_fusion = s32[512]{0:T(512)S(1)} fusion(s32[512]{0:T(512)S(1)} %bitcast.145, s32[1024]{0:T(1024)S(1)} %pad_clamp_fusion), kind=kCustom, calls=%fused_computation | custom fusion | bytes 6144 | tf_op jit(solution)/shard_map/jit(_take)/gather | solution.py:116
  18.6 1.6 collective-permute-start.2
  20.2 15.7 %all-gather = bf16[1,512,512]{1,2,0:T(8,128)(2,1)S(1)} all-gather(bf16[1,128,512]{1,2,0:T(8,128)(2,1)S(1)} %copy.22), channel_id=2, replica_groups=mesh['section'=4,'cp'=4,'tp'=2] {'cp'}, dimensions={1}, use_global_device_ids=true | all-gather | bytes 655360 | tf_op jit(solution)/shard_map/all_gather | solution.py:112
  37.2 5.6 %collective-permute-done.3 = bf16[128,512]{1,0:T(8,128)(2,1)S(1)} collective-permute-done((bf16[128,512]{1,0:T(8,128)(2,1)S(1)}, bf16[128,512]{1,0:T(8,128)(2,1)S(1)}, u32[]{:S(2)}, u32[]{:S(2)}) %collective-permute-start.3) | collective-permute-done | bytes 131104 | tf_op jit(solution)/shard_map/ppermute | solution.py:20
  47.2 1.5 broadcast.133.clone
  48.7 23.3 %while.26 = (s32[]{:T(128)}, bf16[4,1024,512]{1,2,0:T(8,128)(2,1)}, f32[4,1024,128]{2,1,0:T(8,128)}, bf16[4,1024,128]{1,2,0:T(8,128)(2,1)S(1)}, bf16[4,512,128]{...) while((s32[]{:T(128)}, bf16[4,1024,512]{1,2,0:T(8,128)(2,1)}, ...), condition=%wide.region_3.4_spmd.clone, body=%wide.region_0.3_spmd.clone.sunk | while | flops 274397184 | bytes 11701869 | solution.py:124
  50.9 2.3 %fusion.47 = f32[4,1024,128]{2,1,0:T(8,128)} fusion(f32[4,1024,128]{2,1,0:T(8,128)} %get-tuple-element.324, s32[]{:T(128)} %get-tuple-element.322, bf16[4,512,128]{2,1,0:T(8,128)(2,1)} %get-tuple-element.338, f32[1024,512]{0,1:T(8,128)S(1)} %get-tuple-element.309, f32[1024]{0:T(1024)S(1)} %fusion.46, f32[1024]{0:T(1024)S(1)} %get-tuple-element.310), kind=kOutput, calls=%fused_computation.25.clone.1 | convolution fusion | flops 135790592 | bytes 2761728 | tf_op jit(solution)/shard_map/while/body/eval_jaxpr/dot_general | solution.py:65
  54.9 1.5 fusion.45
  56.7 2.3 %fusion.47 = f32[4,1024,128]{2,1,0:T(8,128)} fusion(f32[4,1024,128]{2,1,0:T(8,128)} %get-tuple-element.324, s32[]{:T(128)} %get-tuple-element.322, bf16[4,512,128]{2,1,0:T(8,128)(2,1)} %get-tuple-element.338, f32[1024,512]{0,1:T(8,128)S(1)} %get-tuple-element.309, f32[1024]{0:T(1024)S(1)} %fusion.46, f32[1024]{0:T(1024)S(1)} %get-tuple-element.310), kind=kOutput, calls=%fused_computation.25.clone.1 | convolution fusion | flops 135790592 | bytes 2761728 | tf_op jit(solution)/shard_map/while/body/eval_jaxpr/dot_general | solution.py:65
  62.6 2.2 %fusion.47 = f32[4,1024,128]{2,1,0:T(8,128)} fusion(f32[4,1024,128]{2,1,0:T(8,128)} %get-tuple-element.324, s32[]{:T(128)} %get-tuple-element.322, bf16[4,512,128]{2,1,0:T(8,128)(2,1)} %get-tuple-element.338, f32[1024,512]{0,1:T(8,128)S(1)} %get-tuple-element.309, f32[1024]{0:T(1024)S(1)} %fusion.46, f32[1024]{0:T(1024)S(1)} %get-tuple-element.310), kind=kOutput, calls=%fused_computation.25.clone.1 | convolution fusion | flops 135790592 | bytes 2761728 | tf_op jit(solution)/shard_map/while/body/eval_jaxpr/dot_general | solution.py:65
  66.6 1.5 fusion.45
  68.4 2.2 %fusion.47 = f32[4,1024,128]{2,1,0:T(8,128)} fusion(f32[4,1024,128]{2,1,0:T(8,128)} %get-tuple-element.324, s32[]{:T(128)} %get-tuple-element.322, bf16[4,512,128]{2,1,0:T(8,128)(2,1)} %get-tuple-element.338, f32[1024,512]{0,1:T(8,128)S(1)} %get-tuple-element.309, f32[1024]{0:T(1024)S(1)} %fusion.46, f32[1024]{0:T(1024)S(1)} %get-tuple-element.310), kind=kOutput, calls=%fused_computation.25.clone.1 | convolution fusion | flops 135790592 | bytes 2761728 | tf_op jit(solution)/shard_map/while/body/eval_jaxpr/dot_general | solution.py:65
  76.2 4.8 %fusion.26 = f32[4,512,128]{1,2,0:T(8,128)} fusion(bf16[4,1024,512]{1,2,0:T(8,128)(2,1)} %get-tuple-element.347, bf16[4,1024,128]{1,2,0:T(8,128)(2,1)S(1)} %reshape.165), kind=kOutput, calls=%fused_computation.60 | convolution fusion | flops 536870912 | bytes 6291456 | tf_op jit(solution)/shard_map/vmap()/dot_general | solution.py:88
  82.4 31.5 %while.25 = (s32[]{:T(128)}, bf16[4,1024,512]{2,1,0:T(8,128)(2,1)}, f32[4,1024,128]{2,1,0:T(8,128)}, bf16[4,1024,512]{1,2,0:T(8,128)(2,1)}, bf16[4,1024,128]{1,2...) while((s32[]{:T(128)}, bf16[4,1024,512]{2,1,0:T(8,128)(2,1)}, ...), condition=%wide.region_6.7_spmd, body=%wide.region_4.6_spmd.sunk | while | flops 271055872 | bytes 11283049 | solution.py:130
  85.7 2.4 %bitcast_dynamic-update-slice_fusion.4 = (bf16[4,1024,512]{2,1,0:T(8,128)(2,1)}, bf16[1024,512]{1,0:T(8,128)(2,1)S(1)}) fusion(bf16[4,1024,512]{2,1,0:T(8,128)(2,1)} %get-tuple-element.354, s32[]{:T(128)} %get-tuple-element.353, f32[1024]{0:T(1024)S(1)} %fusion.42, bf16[4,512,128]{2,1,0:T(8,128)(2,1)} %get-tuple-element.367, ...), kind=kOutput, calls=%fused_computation.8.clone.1 | convolution fusion | flops 136314880 | bytes 3544576 | tf_op jit(solution)/shard_map/while/body/eval_jaxpr/dot_general | solution.py:72
  88.1 2.1 %fusion.43 = f32[4,1024,128]{2,1,0:T(8,128)} fusion(f32[4,1024,128]{2,1,0:T(8,128)} %get-tuple-element.355, s32[]{:T(128)} %get-tuple-element.353, bf16[1024,512]{1,0:T(8,128)(2,1)S(1)} %get-tuple-element.298, bf16[4,512,128]{2,1,0:T(8,128)(2,1)} %get-tuple-element.369), kind=kOutput, calls=%fused_computation.7.clone.1 | convolution fusion | flops 134348800 | bytes 1704960 | tf_op jit(solution)/shard_map/while/body/eval_jaxpr/dot_general | solution.py:76
  93.6 2.4 %bitcast_dynamic-update-slice_fusion.4 = (bf16[4,1024,512]{2,1,0:T(8,128)(2,1)}, bf16[1024,512]{1,0:T(8,128)(2,1)S(1)}) fusion(bf16[4,1024,512]{2,1,0:T(8,128)(2,1)} %get-tuple-element.354, s32[]{:T(128)} %get-tuple-element.353, f32[1024]{0:T(1024)S(1)} %fusion.42, bf16[4,512,128]{2,1,0:T(8,128)(2,1)} %get-tuple-element.367, ...), kind=kOutput, calls=%fused_computation.8.clone.1 | convolution fusion | flops 136314880 | bytes 3544576 | tf_op jit(solution)/shard_map/while/body/eval_jaxpr/dot_general | solution.py:72
  96.0 2.1 %fusion.43 = f32[4,1024,128]{2,1,0:T(8,128)} fusion(f32[4,1024,128]{2,1,0:T(8,128)} %get-tuple-element.355, s32[]{:T(128)} %get-tuple-element.353, bf16[1024,512]{1,0:T(8,128)(2,1)S(1)} %get-tuple-element.298, bf16[4,512,128]{2,1,0:T(8,128)(2,1)} %get-tuple-element.369), kind=kOutput, calls=%fused_computation.7.clone.1 | convolution fusion | flops 134348800 | bytes 1704960 | tf_op jit(solution)/shard_map/while/body/eval_jaxpr/dot_general | solution.py:76
  101.5 2.4 %bitcast_dynamic-update-slice_fusion.4 = (bf16[4,1024,512]{2,1,0:T(8,128)(2,1)}, bf16[1024,512]{1,0:T(8,128)(2,1)S(1)}) fusion(bf16[4,1024,512]{2,1,0:T(8,128)(2,1)} %get-tuple-element.354, s32[]{:T(128)} %get-tuple-element.353, f32[1024]{0:T(1024)S(1)} %fusion.42, bf16[4,512,128]{2,1,0:T(8,128)(2,1)} %get-tuple-element.367, ...), kind=kOutput, calls=%fused_computation.8.clone.1 | convolution fusion | flops 136314880 | bytes 3544576 | tf_op jit(solution)/shard_map/while/body/eval_jaxpr/dot_general | solution.py:72
  103.9 2.1 %fusion.43 = f32[4,1024,128]{2,1,0:T(8,128)} fusion(f32[4,1024,128]{2,1,0:T(8,128)} %get-tuple-element.355, s32[]{:T(128)} %get-tuple-element.353, bf16[1024,512]{1,0:T(8,128)(2,1)S(1)} %get-tuple-element.298, bf16[4,512,128]{2,1,0:T(8,128)(2,1)} %get-tuple-element.369), kind=kOutput, calls=%fused_computation.7.clone.1 | convolution fusion | flops 134348800 | bytes 1704960 | tf_op jit(solution)/shard_map/while/body/eval_jaxpr/dot_general | solution.py:76
  109.3 2.4 %bitcast_dynamic-update-slice_fusion.4 = (bf16[4,1024,512]{2,1,0:T(8,128)(2,1)}, bf16[1024,512]{1,0:T(8,128)(2,1)S(1)}) fusion(bf16[4,1024,512]{2,1,0:T(8,128)(2,1)} %get-tuple-element.354, s32[]{:T(128)} %get-tuple-element.353, f32[1024]{0:T(1024)S(1)} %fusion.42, bf16[4,512,128]{2,1,0:T(8,128)(2,1)} %get-tuple-element.367, ...), kind=kOutput, calls=%fused_computation.8.clone.1 | convolution fusion | flops 136314880 | bytes 3544576 | tf_op jit(solution)/shard_map/while/body/eval_jaxpr/dot_general | solution.py:72
  111.7 2.1 %fusion.43 = f32[4,1024,128]{2,1,0:T(8,128)} fusion(f32[4,1024,128]{2,1,0:T(8,128)} %get-tuple-element.355, s32[]{:T(128)} %get-tuple-element.353, bf16[1024,512]{1,0:T(8,128)(2,1)S(1)} %get-tuple-element.298, bf16[4,512,128]{2,1,0:T(8,128)(2,1)} %get-tuple-element.369), kind=kOutput, calls=%fused_computation.7.clone.1 | convolution fusion | flops 134348800 | bytes 1704960 | tf_op jit(solution)/shard_map/while/body/eval_jaxpr/dot_general | solution.py:76
  113.9 3.2 %convolution_multiply_fusion.1 = f32[4,512,128]{1,2,0:T(8,128)S(1)} fusion(bf16[4,1024,128]{1,2,0:T(8,128)(2,1)} %copy-done.3, bf16[4,1024,512]{2,1,0:T(8,128)(2,1)} %get-tuple-element.88), kind=kOutput, calls=%fused_computation.41 | convolution fusion | flops 537133056 | bytes 6291456 | tf_op jit(solution)/shard_map/vmap()/dot_general | solution.py:83
  118.7 1.5 pad_maximum_fusion
  120.2 1.6 copy-done.1
  121.8 2.5 %copy.47 = f32[4,8,128,128]{3,1,0,2:T(8,128)} copy(f32[4,8,128,128]{3,2,1,0:T(8,128)S(1)} %bitcast.147) | data formatting | bytes 4194304 | tf_op jit(solution)/shard_map/reshape | solution.py:46
  124.3 1.7 %reshape.167 = f32[1,128,4096]{2,1,0:T(8,128)S(1)} reshape(f32[128,4,8,128]{3,2,1,0:T(8,128)} %bitcast.148) | data formatting | bytes 4194304 | tf_op jit(solution)/shard_map/reshape | solution.py:48
  126.1 4.1 %copy.48 = f32[4,8,128,128]{3,1,0,2:T(8,128)} copy(f32[4,8,128,128]{3,2,1,0:T(8,128)} %bitcast.23) | data formatting | bytes 4194304 | tf_op jit(solution)/shard_map/reshape | solution.py:46
  130.2 2.8 %reshape.164 = f32[1,128,4096]{2,1,0:T(8,128)} reshape(f32[128,4,8,128]{3,2,1,0:T(8,128)} %bitcast.149) | data formatting | bytes 4194304 | tf_op jit(solution)/shard_map/reshape | solution.py:48
  136.5 24.8 %reduce-scatter.2.cloned.1.call-done = f32[128,1024]{1,0:T(8,128)} async-done(((f32[512,1024]{1,0:T(8,128)}), f32[128,1024]{1,0:T(8,128)}) %reduce-scatter.2.cloned.1.call-update) | async-done | bytes 524304 | tf_op jit(solution)/shard_map/reduce_scatter | solution.py:136
  (96 shorter events, 45.6 us)
Async XLA Ops:
  7.2 7.8 %copy-start = (s32[1,512]{1,0:T(1,128)S(1)}, s32[1,512]{1,0:T(1,128)}, u32[]{:S(2)}) copy-start(s32[1,512]{1,0:T(1,128)} %param.14) | copy-start | bytes 6148
  7.2 35.6 %copy-start.10 = (bf16[1,128,512]{2,1,0:T(8,128)(2,1)S(1)}, bf16[1,128,512]{2,1,0:T(8,128)(2,1)}, u32[]{:S(2)}) copy-start(bf16[1,128,512]{2,1,0:T(8,128)(2,1)} %param.12) | copy-start | bytes 393220
  7.2 11.3 %copy-start.9 = (s32[1,512]{1,0:T(1,128)S(1)}, s32[1,512]{1,0:T(1,128)}, u32[]{:S(2)}) copy-start(s32[1,512]{1,0:T(1,128)} %param.15) | copy-start | bytes 6148
  7.2 154.1 %reduce-scatter.2.cloned.1.call-start = ((), (), s32[]{:S(2)}) async-start(), calls=%async_computation.1 | async-start | bytes 2621440 | tf_op jit(solution)/shard_map/reduce_scatter | solution.py:136
  7.2 11.3 %collective-permute-start.1 = (bf16[128,512]{1,0:T(8,128)(2,1)}, bf16[128,512]{1,0:T(8,128)(2,1)S(1)}, u32[]{:S(2)}, u32[]{:S(2)}) collective-permute-start(bf16[128,512]{1,0:T(8,128)(2,1)} %bitcast.162), channel_id=1, source_target_pairs={{0,2},{2,4},{4,6},{6,0},{1,3},{3,5},{5,7},{7,1},{8,10},{10,12},{12... | collective-permute-start | bytes 393224 | tf_op jit(solution)/shard_map/ppermute | solution.py:20
  10.4 34.1 %collective-permute-start = (bf16[1,128,4096]{2,1,0:T(8,128)(2,1)}, bf16[1,128,4096]{2,1,0:T(8,128)(2,1)S(1)}, u32[]{:S(2)}, u32[]{:S(2)}) collective-permute-start(bf16[1,128,4096]{2,1,0:T(8,128)(2,1)} %param.10), channel_id=1, source_target_pairs={{24,0},{0,8},{8,16},{16,24},{25,1},{1,9},{9,17},{17,25},{26,2},{2,... | collective-permute-start | bytes 3145736 | tf_op jit(solution)/shard_map/ppermute | solution.py:29
  11.8 60.1 %collective-permute-start.4 = (bf16[1,128,4096]{2,1,0:T(8,128)(2,1)}, bf16[1,128,4096]{2,1,0:T(8,128)(2,1)S(1)}, u32[]{:S(2)}, u32[]{:S(2)}) collective-permute-start(bf16[1,128,4096]{2,1,0:T(8,128)(2,1)} %param.13), channel_id=1, source_target_pairs={{8,0},{16,8},{24,16},{0,24},{9,1},{17,9},{25,17},{1,25},{10,2},{18... | collective-permute-start | bytes 3145736 | tf_op jit(solution)/shard_map/ppermute | solution.py:29
  18.6 17.4 %collective-permute-start.2 = (bf16[128,512]{1,0:T(8,128)(2,1)S(1)}, bf16[128,512]{1,0:T(8,128)(2,1)S(1)}, u32[]{:S(2)}, u32[]{:S(2)}) collective-permute-start(bf16[128,512]{1,0:T(8,128)(2,1)S(1)} %collective-permute-done.1), channel_id=1, source_target_pairs={{0,2},{2,4},{4,6},{6,0},{1,3},{3,5},{5,7},{7,1},{8,10},{10,12},{12... | collective-permute-start | bytes 393224 | tf_op jit(solution)/shard_map/ppermute | solution.py:20
  36.0 6.8 %collective-permute-start.3 = (bf16[128,512]{1,0:T(8,128)(2,1)S(1)}, bf16[128,512]{1,0:T(8,128)(2,1)S(1)}, u32[]{:S(2)}, u32[]{:S(2)}) collective-permute-start(bf16[128,512]{1,0:T(8,128)(2,1)S(1)} %collective-permute-done.2), channel_id=1, source_target_pairs={{0,2},{2,4},{4,6},{6,0},{1,3},{3,5},{5,7},{7,1},{8,10},{10,12},{12... | collective-permute-start | bytes 393224 | tf_op jit(solution)/shard_map/ppermute | solution.py:20
  44.5 1.0 copy-start.4
  72.0 3.7 %copy-start.3 = (bf16[4,1024,128]{1,2,0:T(8,128)(2,1)}, bf16[4,1024,128]{1,2,0:T(8,128)(2,1)S(1)}, u32[]{:S(2)}) copy-start(bf16[4,1024,128]{1,2,0:T(8,128)(2,1)S(1)} %get-tuple-element.374) | copy-start | bytes 3145732
  72.0 1.0 copy-start.6
  117.1 1.2 copy-start.8
  120.2 1.6 copy-start.1
  130.2 2.9 %copy-start.7 = (bf16[1,128,4096]{2,1,0:T(8,128)(2,1)S(1)}, bf16[1,128,4096]{2,1,0:T(8,128)(2,1)}, u32[]{:S(2)}) copy-start(bf16[1,128,4096]{2,1,0:T(8,128)(2,1)} %copy-done.6) | copy-start | bytes 3145732
  133.1 2.0 %copy-start.2 = (f32[1,128,4096]{2,1,0:T(8,128)S(1)}, f32[1,128,4096]{2,1,0:T(8,128)}, u32[]{:S(2)}) copy-start(f32[1,128,4096]{2,1,0:T(8,128)} %reshape.164) | copy-start | bytes 6291460
  133.1 2.2 %copy-start.5 = (bf16[1,128,4096]{2,1,0:T(8,128)(2,1)S(1)}, bf16[1,128,4096]{2,1,0:T(8,128)(2,1)}, u32[]{:S(2)}) copy-start(bf16[1,128,4096]{2,1,0:T(8,128)(2,1)} %copy-done.4) | copy-start | bytes 3145732
Sparse Core Ops, SparseCore 0:
  120.4 40.9 reduce-scatter.1
